TPU v7x, 32 devices: a whole 2x2x4 slice. The times are simulated.
32 devices in a mesh: fsdp: 16 (over z, y, x), dp: 2 (over core).
Axes of the slice: x: 2, y: 2, z: 4, core: 2. Of those that a mesh axis runs over, the one named last changes fastest.
Arguments:
- normed: bfloat16 [2, 4096, 4096], P(None, ('fsdp', 'dp')), may hold values from -6 to 6
- kv_cotangent: bfloat16 [2, 4096, 512], P(None, ('fsdp', 'dp')), may hold values from -6 to 6
- kv_weight: bfloat16 [4096, 512], P('fsdp'), may hold values from -0.09375 to 0.09375
- main_grad: float32 [4096, 512], P('fsdp'), may hold values from -6 to 6
- owner_order: int32 [16], replicated, may hold values from 0 to 15, each once
Outputs:
- key_rows: bfloat16 [2, 4096, 512], P(None, ('fsdp', 'dp'))
- input_grad: bfloat16 [2, 4096, 4096], P(None, ('fsdp', 'dp'))
- grad_buffer: float32 [4096, 512], P('fsdp')
Inputs may be any that keep to these rules, and one draw needn't show every extreme that they name: `owner_order`: a permutation: each value appears once.
All inputs are finite; a program needn't handle non-finite values.
Results may differ from a plain program's by a relative error of at most 0.0075.
Values may be sent and summed in bfloat16 or wider, within the bound.
A program may use at most 64 MiB of HBM per device.

v0:
```python
import math
import jax
import jax.numpy as jnp
from jax import lax
from jax.sharding import PartitionSpec as P


def term_from(inputs, cotangent):

    def gradient_term(first_row, row_count):
        return lax.dot_general(
            inputs, cotangent, (((0,), (0,)), ((), ())), preferred_element_type=jnp.float32
        )

    return gradient_term


def body(normed, kv_cotangent, kv_weight, main_grad, owner_order):
    micro_count, tok_dev, width = normed.shape
    shard_rows, key_width = kv_weight.shape
    owners = lax.axis_size("fsdp")
    everyone = owners * lax.axis_size("dp")
    all_rows = micro_count * tok_dev
    permuted = jnp.take(normed.reshape(all_rows, owners, shard_rows), owner_order, axis=1).reshape(
        all_rows, width
    )
    flat_cot = kv_cotangent.reshape(all_rows, key_width)
    gathered = lax.all_gather(kv_weight, "fsdp", axis=0, tiled=True)
    key_sum = jnp.dot(permuted, gathered, preferred_element_type=jnp.float32)
    grad_permuted = lax.dot_general(
        flat_cot, gathered, (((1,), (1,)), ((), ())), preferred_element_type=jnp.float32
    ).astype(jnp.bfloat16)
    indices = jnp.arange(owners, dtype=jnp.int32)
    inverse_owner = jnp.sum(
        jnp.where(owner_order[None, :] == indices[:, None], indices[None, :], 0), axis=1
    )
    input_grad = jnp.take(
        grad_permuted.reshape(all_rows, owners, shard_rows), inverse_owner, axis=1
    ).reshape(micro_count, tok_dev, width)
    shard_sum = jnp.zeros((shard_rows, key_width), jnp.float32)
    for micro_index in range(micro_count):
        lower = micro_index * tok_dev
        upper = lower + tok_dev
        gradient_term = term_from(permuted[lower:upper], flat_cot[lower:upper])
        shard_sum = shard_sum + lax.psum_scatter(
            gradient_term(jnp.int32(0), shard_rows * lax.axis_size("fsdp")),
            "fsdp",
            scatter_dimension=0,
            tiled=True,
        )
    replica_total = lax.psum(shard_sum.astype(jnp.bfloat16), "dp").astype(jnp.float32)
    grad_scale = 1.0 / math.sqrt(micro_count * tok_dev * everyone)
    grad_buffer = main_grad + replica_total * grad_scale
    key_rows = key_sum.astype(jnp.bfloat16).reshape(micro_count, tok_dev, key_width)
    return (key_rows, input_grad, grad_buffer)


def solution(mesh):
    in_specs = (
        P(None, ("fsdp", "dp"), None),
        P(None, ("fsdp", "dp"), None),
        P("fsdp", None),
        P("fsdp", None),
        P(),
    )
    out_specs = (P(None, ("fsdp", "dp"), None), P(None, ("fsdp", "dp"), None), P("fsdp", None))
    return jax.shard_map(body, mesh=mesh, in_specs=in_specs, out_specs=out_specs, check_vma=False)
```

profile of v0, /device:TPU:0, one launch (start us, length us, event | category | flops | bytes accessed | tf_op | source)
XLA Modules:
  0.0 299.8 jit_solution(3278835918470781926)
XLA Ops:
  7.2 0.0 all-gather.2.cloned.1.call-start
  7.2 0.7 all-gather.2.cloned.1.call-update
  7.9 0.0 reduce-scatter.2.cloned.1.call-start
  7.9 2.2 copy.22
  10.2 0.0 copy-start.3
  10.2 0.7 copy.15
  10.9 0.0 copy-done.3
  10.9 2.0 gather_fusion
  12.9 1.8 select_bitcast_fusion.1
  14.8 1.5 fusion.5
  16.3 0.0 copy-start.1
  16.3 1.7 copy.19
  17.9 2.3 copy.20
  20.2 0.0 copy-done.1
  20.2 0.0 copy-start
  20.2 1.2 fusion.1
  21.4 0.0 copy-done
  21.5 4.5 %convolution_add_fusion = f32[4096,512]{1,0:T(8,128)} fusion(f32[4096,512]{1,0:T(8,128)S(1)} %fusion.1, bf16[128,4096]{0,1:T(8,128)(2,1)S(1)} %bitcast.32, bf16[2,128,512]{2,1,0:T(8,128)(2,1)S(1)} %copy-done.1), kind=kOutput, calls=%fused_computation.2 | convolution fusion | flops 538968064 | bytes 17956864 | tf_op jit(solution)/shard_map/dot_general | solution.py:11
  25.9 0.0 reduce-scatter.2.cloned.1.call-update
  25.9 0.0 all-reduce.2.cloned.1.call-start
  26.0 2.4 copy.16
  28.4 0.1 select_reduce_fusion
  28.6 60.5 %all-gather.2.cloned.1.call-done = bf16[4096,512]{1,0:T(8,128)(2,1)} async-done(((bf16[256,512]{1,0:T(8,128)(2,1)}), bf16[4096,512]{1,0:T(8,128)(2,1)}) %all-gather.2.cloned.1.call-update) | async-done | bytes 4194320 | tf_op jit(solution)/shard_map/all_gather | solution.py:28
  89.1 3.5 %convolution_convert_fusion = bf16[256,4096]{1,0:T(8,128)(2,1)S(1)} fusion(bf16[256,512]{1,0:T(8,128)(2,1)S(1)} %bitcast.35, bf16[4096,512]{1,0:T(8,128)(2,1)} %all-gather.2.cloned.1.call-done), kind=kOutput, calls=%fused_computation.3 | convolution fusion | flops 1074790400 | bytes 6553600 | tf_op jit(solution)/shard_map/dot_general | solution.py:30
  92.6 1.5 copy.24
  94.1 2.3 gather_fusion.1
  96.4 0.3 select_bitcast_fusion
  96.7 1.2 copy.18
  97.8 2.3 reshape.39
  100.2 167.7 %reduce-scatter.2.cloned.1.call-done = f32[256,512]{1,0:T(8,128)} async-done(((f32[4096,512]{1,0:T(8,128)}), f32[256,512]{1,0:T(8,128)}) %reduce-scatter.2.cloned.1.call-update) | async-done | bytes 524304 | tf_op jit(solution)/shard_map/reduce_scatter | solution.py:45
  267.9 1.8 convert_element_type.14
  269.7 0.0 all-reduce.2.cloned.1.call-update
  269.7 0.0 copy-start.2
  269.7 4.8 %convolution_convert_fusion.1 = bf16[256,512]{1,0:T(8,128)(2,1)} fusion(bf16[256,4096]{0,1:T(8,128)(2,1)} %bitcast.34, bf16[4096,512]{1,0:T(8,128)(2,1)} %all-gather.2.cloned.1.call-done), kind=kOutput, calls=%fused_computation.7 | convolution fusion | flops 1073872896 | bytes 6553600 | tf_op jit(solution)/shard_map/dot_general | solution.py:29
  274.5 16.9 %all-reduce.2.cloned.1.call-done = bf16[256,512]{1,0:T(8,128)(2,1)} async-done(((bf16[256,512]{1,0:T(8,128)(2,1)}), bf16[256,512]{1,0:T(8,128)(2,1)}) %all-reduce.2.cloned.1.call-update) | async-done | bytes 262160 | tf_op jit(solution)/shard_map/psum | solution.py:51
  291.5 0.0 copy-done.2
  291.5 1.8 multiply_add_fusion
  (6 shorter events, 0.0 us)
Async XLA Ops:
  7.2 81.9 %all-gather.2.cloned.1.call-start = ((), (), s32[]{:S(2)}) async-start(), calls=%async_computation.1 | async-start | bytes 4456448 | tf_op jit(solution)/shard_map/all_gather | solution.py:28
  7.9 260.0 %reduce-scatter.2.cloned.1.call-start = ((), (), s32[]{:S(2)}) async-start(), calls=%async_computation.3 | async-start | bytes 8912896 | tf_op jit(solution)/shard_map/reduce_scatter | solution.py:45
  10.2 0.7 copy-start.3
  16.3 3.9 %copy-start.1 = (bf16[2,128,512]{2,1,0:T(8,128)(2,1)S(1)}, bf16[2,128,512]{2,1,0:T(8,128)(2,1)}, u32[]{:S(2)}) copy-start(bf16[2,128,512]{2,1,0:T(8,128)(2,1)} %param.8) | copy-start | bytes 786436
  20.2 1.3 copy-start
  25.9 265.5 %all-reduce.2.cloned.1.call-start = ((), (), s32[]{:S(2)}) async-start(), calls=%async_computation.2 | async-start | bytes 524288 | tf_op jit(solution)/shard_map/psum | solution.py:51
  269.7 21.8 %copy-start.2 = (f32[256,512]{1,0:T(8,128)S(1)}, f32[256,512]{1,0:T(8,128)}, u32[]{:S(2)}) copy-start(f32[256,512]{1,0:T(8,128)} %param.10) | copy-start | bytes 1572868
Sparse Core Ops, SparseCore 0:
  10.7 78.3 all-gather.1
  91.4 176.4 reduce-scatter.1
  270.8 20.6 all-reduce.1
where the time goes:
time: 300 us
  waiting for transfers between devices  246 us (82%)
  local copies, waits for them, and re-layouts  20.1 us (7%)
  matrix products  14 us (5%)
  between operations  13.9 us (5%)
  other arithmetic  5.86 us (2%)
    reduce_scatter x1, waiting for transfers between devices, body(): lax.psum_scatter(gradient_term(jnp.int32(0), shard_rows * lax.axis_size('...  168 us
    all_gather x1, waiting for transfers between devices, body(): gathered = lax.all_gather(kv_weight, 'fsdp', axis=0, tiled=True)  60.5 us
    psum x1, waiting for transfers between devices, body(): lax.psum(shard_sum.astype(jnp.bfloat16), 'dp').astype(jnp.float32)  16.9 us
  transfers between devices with their start and end apart: 3, of which 3 were waited for; matrix products, arithmetic and copies ran while one was open for 12% of the time, Pallas kernels for 0%

commit v1 on v0

--- a/solution.py
+++ b/solution.py
@@ -48,7 +48,9 @@
             scatter_dimension=0,
             tiled=True,
         )
-    replica_total = lax.psum(shard_sum.astype(jnp.bfloat16), "dp").astype(jnp.float32)
+    replica_total = jnp.sum(lax.all_gather(shard_sum.astype(jnp.bfloat16), "dp"), axis=0).astype(
+        jnp.float32
+    )
     grad_scale = 1.0 / math.sqrt(micro_count * tok_dev * everyone)
     grad_buffer = main_grad + replica_total * grad_scale
     key_rows = key_sum.astype(jnp.bfloat16).reshape(micro_count, tok_dev, key_width)

time: 300 us -> 281 us (0.937)
  waiting for transfers between devices: 246 us -> 224 us
    psum x1 -> x0, waiting for transfers between devices: 16.9 us -> none  [body(): lax.psum(shard_sum.astype(jnp.bfloat16), 'dp').astype(jnp.float32)]
    reduce_scatter x1, waiting for transfers between devices: 168 us -> 163 us  [body(): lax.psum_scatter(gradient_term(jnp.int32(0), shard_rows * lax.axis_size('...]
  transfers between devices with their start and end apart: 3 -> 2, of which waited for: 3 -> 2; matrix products, arithmetic and copies ran while one was open for 12% -> 13% of each run, Pallas kernels for 0% -> 0%
where the time goes in v1:
time: 281 us; the launch traced here: 279 us
  waiting for transfers between devices  224 us (80%)
  local copies, waits for them, and re-layouts  20.1 us (7%)
  between operations  14.2 us (5%)
  matrix products  13.9 us (5%)
  other arithmetic  4.3 us (2%)
    reduce_scatter x1, waiting for transfers between devices, body(): lax.psum_scatter(gradient_term(jnp.int32(0), shard_rows * lax.axis_size('...  163 us
    all_gather x1, waiting for transfers between devices, body(): gathered = lax.all_gather(kv_weight, 'fsdp', axis=0, tiled=True)  60.6 us
    dot_general x2, matrix products, gradient_term(): lax.dot_general(inputs, cotangent, (((0,), (0,)), ((), ())), preferred_el...  5.68 us
  transfers between devices with their start and end apart: 2, of which 2 were waited for; matrix products, arithmetic and copies ran while one was open for 13% of the time, Pallas kernels for 0%

profile of v1, /device:TPU:0, one launch (start us, length us, event | category | flops | bytes accessed | tf_op | source)
XLA Modules:
  0.0 278.9 jit_solution(8774011712075594072)
XLA Ops:
  7.2 0.0 all-gather.3.cloned.1.call-start
  7.2 0.7 all-gather.3.cloned.1.call-update
  7.9 0.0 reduce-scatter.2.cloned.1.call-start
  7.9 2.2 copy.22
  10.2 0.0 copy-start.3
  10.2 0.7 copy.15
  10.9 0.0 copy-done.3
  10.9 2.0 gather_fusion
  12.9 1.8 select_bitcast_fusion.1
  14.8 1.5 fusion.5
  16.3 0.0 copy-start.1
  16.3 1.7 copy.19
  17.9 2.3 copy.20
  20.2 0.0 copy-done.1
  20.2 0.0 copy-start
  20.2 1.2 fusion.1
  21.4 0.0 copy-done
  21.5 4.5 %convolution_add_fusion = f32[4096,512]{1,0:T(8,128)} fusion(f32[4096,512]{1,0:T(8,128)S(1)} %fusion.1, bf16[128,4096]{0,1:T(8,128)(2,1)S(1)} %bitcast.33, bf16[2,128,512]{2,1,0:T(8,128)(2,1)S(1)} %copy-done.1), kind=kOutput, calls=%fused_computation.2 | convolution fusion | flops 538968064 | bytes 17956864 | tf_op jit(solution)/shard_map/dot_general | solution.py:11
  25.9 0.0 reduce-scatter.2.cloned.1.call-update
  25.9 2.4 copy.16
  28.4 0.1 select_reduce_fusion
  28.5 60.6 %all-gather.3.cloned.1.call-done = bf16[4096,512]{1,0:T(8,128)(2,1)} async-done(((bf16[256,512]{1,0:T(8,128)(2,1)}), bf16[4096,512]{1,0:T(8,128)(2,1)}) %all-gather.3.cloned.1.call-update) | async-done | bytes 4194320 | tf_op jit(solution)/shard_map/all_gather | solution.py:28
  89.1 3.5 %convolution_convert_fusion = bf16[256,4096]{1,0:T(8,128)(2,1)S(1)} fusion(bf16[256,512]{1,0:T(8,128)(2,1)S(1)} %bitcast.37, bf16[4096,512]{1,0:T(8,128)(2,1)} %all-gather.3.cloned.1.call-done), kind=kOutput, calls=%fused_computation.3 | convolution fusion | flops 1074790400 | bytes 6553600 | tf_op jit(solution)/shard_map/dot_general | solution.py:30
  92.6 1.5 copy.24
  94.1 2.3 gather_fusion.1
  96.4 0.3 select_bitcast_fusion
  96.7 1.2 copy.18
  97.8 2.3 reshape.39
  100.2 4.8 %convolution_convert_fusion.1 = bf16[256,512]{1,0:T(8,128)(2,1)} fusion(bf16[256,4096]{0,1:T(8,128)(2,1)} %bitcast.35, bf16[4096,512]{1,0:T(8,128)(2,1)} %all-gather.3.cloned.1.call-done), kind=kOutput, calls=%fused_computation.7 | convolution fusion | flops 1073872896 | bytes 6553600 | tf_op jit(solution)/shard_map/dot_general | solution.py:29
  105.0 0.0 copy-start.2
  105.0 162.9 %reduce-scatter.2.cloned.1.call-done = f32[256,512]{1,0:T(8,128)} async-done(((f32[4096,512]{1,0:T(8,128)}), f32[256,512]{1,0:T(8,128)}) %reduce-scatter.2.cloned.1.call-update) | async-done | bytes 524304 | tf_op jit(solution)/shard_map/reduce_scatter | solution.py:45
  267.9 1.1 convert_element_type.16
  269.0 2.2 all-gather
  271.1 0.1 reduce_sum.22
  271.2 0.0 copy-done.2
  271.2 0.9 multiply_add_fusion
  (6 shorter events, 0.0 us)
Async XLA Ops:
  7.2 81.9 %all-gather.3.cloned.1.call-start = ((), (), s32[]{:S(2)}) async-start(), calls=%async_computation.1 | async-start | bytes 4456448 | tf_op jit(solution)/shard_map/all_gather | solution.py:28
  7.9 260.0 %reduce-scatter.2.cloned.1.call-start = ((), (), s32[]{:S(2)}) async-start(), calls=%async_computation.2 | async-start | bytes 8912896 | tf_op jit(solution)/shard_map/reduce_scatter | solution.py:45
  10.2 0.7 copy-start.3
  16.3 3.9 %copy-start.1 = (bf16[2,128,512]{2,1,0:T(8,128)(2,1)S(1)}, bf16[2,128,512]{2,1,0:T(8,128)(2,1)}, u32[]{:S(2)}) copy-start(bf16[2,128,512]{2,1,0:T(8,128)(2,1)} %param.8) | copy-start | bytes 786436
  20.2 1.3 copy-start
  105.0 166.3 %copy-start.2 = (f32[256,512]{1,0:T(8,128)S(1)}, f32[256,512]{1,0:T(8,128)}, u32[]{:S(2)}) copy-start(f32[256,512]{1,0:T(8,128)} %param.10) | copy-start | bytes 1572868
Sparse Core Ops, SparseCore 0:
  10.7 78.3 all-gather.2
  91.4 176.4 reduce-scatter.1
